TPU v7x, 32 devices: a whole 2x2x4 slice. The times are simulated.
32 devices in a mesh: seq: 8 (over z, y), head: 4 (over x, core).
Axes of the slice: x: 2, y: 2, z: 4, core: 2. Of those that a mesh axis runs over, the one named last changes fastest.
Arguments:
- query_rows: bfloat16 [4096, 4096], P('seq', 'head'), may hold values from -6 to 6
- key_rows: bfloat16 [4096, 4096], P('seq', 'head'), may hold values from -2 to 2
- value_rows: bfloat16 [4096, 4096], P('seq', 'head'), may hold values from -6 to 6
- key_gain: float32 [32], P('head'), may hold values from 0.9 to 1.85, as said below
- regularizer: float32 [32], P('head'), may hold values from 0.5 to 4
Outputs:
- readout: bfloat16 [4096, 4096], P('seq', 'head')
Inputs may be any that keep to these rules, and one draw needn't show every extreme that they name: `key_gain`: one positive gain for each head.
All inputs are finite; a program needn't handle non-finite values.
Results may differ from a plain program's by a relative error of at most 0.006.
Values sent between devices are 32-bit elements; how exact they have to be, the bound alone decides.
A program may use at most 192 MiB of HBM per device.

v0:
```python
import functools

import jax
import jax.numpy as jnp
from jax import lax
from jax.experimental import pallas as pl
from jax.experimental.pallas import tpu as pltpu
from jax.sharding import PartitionSpec as P

NS_STEPS = 8
REFINE = 2
LANES = 2
F32 = jnp.float32
BF16 = jnp.bfloat16
MESH = pl.DeviceIdType.MESH


def mm(left, right):
    return lax.dot_general(left, right, (((1,), (0,)), ((), ())), preferred_element_type=F32)


def mm_nt(left, right):
    return lax.dot_general(left, right, (((1,), (1,)), ((), ())), preferred_element_type=F32)


def mm_tn(left, right):
    return lax.dot_general(left, right, (((0,), (0,)), ((), ())), preferred_element_type=F32)


def halves(value):
    high = value.astype(BF16)
    low = (value - high.astype(F32)).astype(BF16)
    return jnp.concatenate([high, low], axis=1)


def fold(wide):
    width = wide.shape[1] // 2
    return wide[:, :width] + wide[:, width:]


def twice(pair):
    return jnp.concatenate([pair, pair], axis=0)


def kernel(
    chain,
    gain_ref, ridge_ref, query_hbm, key_hbm, value_hbm, out_ref,
    query_ref, key_ref, value_ref,
    keys, turned_keys, gram_head, gram_all, cross_head, cross_all,
    gram_in, gram_out, gram_side, cross_in, cross_out, cross_mix, cross_half, cross_side,
    weights, start, solved, final,
    query_sem, key_sem, value_sem,
    gram_send, gram_recv, side_send, side_recv,
    cross_send, cross_recv, half_send, half_recv, cside_send, cside_recv,
):
    heads = keys.shape[0]
    tokens, dim = keys.shape[1:]
    sub = tokens // 2
    pairs = heads // 2
    place = lax.axis_index("seq")
    row, lane = place // LANES, place % LANES
    partner = place + 1 - 2 * lane
    has_prev, has_next = row > 0, row < chain - 1
    gets_side = jnp.logical_or(lane == 1, has_prev)

    barrier = pltpu.get_barrier_semaphore()

    def greet(device):
        pl.semaphore_signal(barrier, inc=1, device_id={"seq": device}, device_id_type=MESH)

    greet(partner)

    @pl.when(has_prev)
    def _():
        greet(place - LANES)

    @pl.when(has_next)
    def _():
        greet(place + LANES)

    def pair_cols(p):
        return slice(2 * p * dim, 2 * (p + 1) * dim)

    def fetch(p, src, dst, sem):
        return pltpu.make_async_copy(src.at[:, pair_cols(p)], dst.at[:, pair_cols(p)], sem.at[p])

    for p in range(pairs):
        fetch(p, key_hbm, key_ref, key_sem).start()
    for p in range(pairs):
        fetch(p, value_hbm, value_ref, value_sem).start()
    for p in range(pairs):
        fetch(p, query_hbm, query_ref, query_sem).start()

    i = lax.broadcasted_iota(jnp.int32, (dim, dim), 0)
    j = lax.broadcasted_iota(jnp.int32, (dim, dim), 1)
    eye = jnp.where(i == j, 1.0, 0.0).astype(F32)

    def copy(src, dst, send, recv, device):
        return pltpu.make_async_remote_copy(
            src_ref=src, dst_ref=dst, send_sem=send, recv_sem=recv,
            device_id={"seq": device}, device_id_type=MESH,
        )

    pieces = [(p, q) for p in range(pairs) for q in range(2)]
    spans = (slice(0, dim // 2), slice(dim // 2, dim + 8))

    def gram_next(p, q):
        n = 2 * p + q
        return copy(
            gram_out.at[p, spans[q]], gram_in.at[p, spans[q]],
            gram_send.at[n], gram_recv.at[n], place + LANES,
        )

    def gram_across(p, q, src):
        n = 2 * p + q
        return copy(
            src.at[p, spans[q]], gram_side.at[p, spans[q]],
            side_send.at[n], side_recv.at[n], partner,
        )

    def cross_next(p):
        return copy(cross_out.at[p], cross_in.at[p], cross_send.at[p], cross_recv.at[p], place + LANES)

    def cross_across(p, src):
        return copy(src.at[p], cross_side.at[p], cside_send.at[p], cside_recv.at[p], partner)

    def send_gram(p, q):
        @pl.when(has_next)
        def _():
            gram_next(p, q).start()

        @pl.when(lane == 0)
        def _():
            gram_across(p, q, gram_out).start()

    def cross_swap(p):
        return copy(
            cross_all.at[2 * p + 1 - lane], cross_half.at[p],
            half_send.at[p], half_recv.at[p], partner,
        )

    def relay_cross(p):
        cross_swap(p).wait_recv()

        @pl.when(has_prev)
        def _():
            cross_next(p).wait_recv()

            @pl.when(lane == 1)
            def _():
                cross_across(p, cross_in).start()

        mixed = cross_in[p] + cross_all[2 * p + lane]

        @pl.when(lane == 0)
        def _():
            cross_mix[p] = mixed
            cross_across(p, cross_mix).start()

        @pl.when(has_next)
        def _():
            cross_out[p] = mixed + cross_half[p]
            cross_next(p).start()

    for p in range(pairs):
        fetch(p, key_hbm, key_ref, key_sem).wait()
        for h in (2 * p, 2 * p + 1):
            raw = key_ref[:, h * dim : (h + 1) * dim].astype(F32)
            scaled = (raw * gain_ref[h]).astype(BF16)
            turned = scaled.T
            keys[h] = scaled
            turned_keys[h] = turned
            first = mm(turned[:, :sub], scaled[:sub])
            gram_head[h] = first
            gram_all[h] = first + mm(turned[:, sub:], scaled[sub:])
        upper, lower = gram_all[2 * p], gram_all[2 * p + 1]
        gram_out[p, :dim] = jnp.where(i <= j, upper, lower)
        diagonal = jnp.sum(jnp.where(i == j, lower, 0.0), axis=0, keepdims=True)
        gram_out[p, dim:] = jnp.broadcast_to(diagonal, (8, dim))
        if p == 0:
            pl.semaphore_wait(barrier, 1 + has_prev.astype(jnp.int32) + has_next.astype(jnp.int32))

        @pl.when(jnp.logical_not(has_prev))
        def _():
            for q in range(2):
                send_gram(p, q)

    for p in range(pairs):
        fetch(p, value_hbm, value_ref, value_sem).wait()
        for h in (2 * p, 2 * p + 1):
            values = value_ref[:, h * dim : (h + 1) * dim]
            first = mm(turned_keys[h, :, :sub], values[:sub])
            total = first + mm(turned_keys[h, :, sub:], values[sub:])
            cross_head[h] = first
            cross_all[h] = total
        cross_swap(p).start()

    @pl.when(jnp.logical_not(has_prev))
    def _():
        gram_in[...] = jnp.zeros_like(gram_in)
        cross_in[...] = jnp.zeros_like(cross_in)
        for p in range(pairs):
            relay_cross(p)

    @pl.when(jnp.logical_not(gets_side))
    def _():
        gram_side[...] = jnp.zeros_like(gram_side)
        cross_side[...] = jnp.zeros_like(cross_side)

    for p in range(pairs):
        fetch(p, query_hbm, query_ref, query_sem).wait()

    @pl.when(has_prev)
    def _():
        for p, q in pieces:
            gram_next(p, q).wait_recv()

            @pl.when(lane == 1)
            def _():
                gram_across(p, q, gram_in).start()

            gram_out[p, spans[q]] += gram_in[p, spans[q]]
            send_gram(p, q)

    def arrive(p):
        @pl.when(gets_side)
        def _():
            for q in range(2):
                gram_across(p, q, gram_in).wait_recv()

    def precondition(p, result):
        packed = gram_in[p] + gram_side[p]
        square = packed[:dim]
        turned = square.T
        upper = jnp.where(i <= j, square, turned)
        lower = jnp.where(i > j, square, jnp.where(i < j, turned, packed[dim : dim + 1]))
        state = []
        for h, prior in ((2 * p, upper), (2 * p + 1, lower)):
            plain = ridge_ref[h] * eye + prior
            gram_head[h] = plain + gram_head[h]
            end = plain + gram_all[h]
            gram_all[h] = plain
            total = jnp.sum(jnp.sum(end * end, axis=1, keepdims=True), axis=0, keepdims=True)
            inverse = 1.0 / jnp.sqrt(total)
            rest = eye - end * inverse
            split = halves(rest)
            both = jnp.concatenate([eye + rest, fold(mm(split, twice(split)))], axis=0)
            state.append((both, inverse))
        yield
        for step in range(NS_STEPS - 2):
            for k in range(2):
                both, inverse = state[k]
                split = halves(both)
                product = fold(mm(split, twice(split[dim:])))
                both = jnp.concatenate([both[:dim] + product[:dim], product[dim:]], axis=0)
                state[k] = (both, inverse)
            yield
        for both, inverse in state:
            split = halves(both)
            approx = both[:dim] + fold(mm(split[:dim], twice(split[dim:])))
            result.append(halves(approx * inverse))
        yield

    t = lax.broadcasted_iota(jnp.int32, (sub, sub), 0)
    u = lax.broadcasted_iota(jnp.int32, (sub, sub), 1)
    causal = t >= u

    def solve(p, preconds):
        slot = p % 2
        for k in range(2):
            h = 2 * p + k
            precond = preconds[k]
            start[slot, k] = fold(mm(query_ref[:, h * dim : (h + 1) * dim], precond))
            shifted = halves(-fold(mm(keys[h], precond)))
            for s, matrix in ((0, gram_all), (1, gram_head)):
                rest = halves(eye - fold(mm(halves(matrix[h]), twice(precond))))
                weights[slot, k, s, :sub] = shifted[s * sub : (s + 1) * sub]
                weights[slot, k, s, sub:] = twice(rest)
            yield
        chains = [(k, s) for k in range(2) for s in range(2)]
        current = {(k, s): start[slot, k, s * sub : (s + 1) * sub] for k, s in chains}
        for repeat in range(REFINE):
            for k, s in chains:
                rows = slice(s * sub, (s + 1) * sub)
                split = halves(current[k, s])
                scores = mm(split[:, :dim], turned_keys[2 * p + k, :, rows])
                scores = jnp.where(causal, scores, 0.0).astype(BF16)
                update = mm(jnp.concatenate([scores, split], axis=1), weights[slot, k, s])
                current[k, s] = start[slot, k, rows] + fold(update)
                if s == 1:
                    yield
        for k, s in chains:
            solved[2 * p + k, s * sub : (s + 1) * sub] = halves(current[k, s])

    def weave(*streams):
        streams = list(streams)
        while streams:
            streams = [stream for stream in streams if next(stream, 0) is None]

    def relay_at(stage):
        early = {0: (0, 1), 1: (2,), 2: range(3, pairs)}
        late = {1: (0,), 2: (1,), 3: range(2, pairs)}
        mine, spare = early.get(stage, ()), late.get(stage, ())

        @pl.when(jnp.logical_and(has_prev, has_next))
        def _():
            for p in mine:
                if p < pairs:
                    relay_cross(p)

        @pl.when(jnp.logical_and(has_prev, jnp.logical_not(has_next)))
        def _():
            for p in spare:
                if p < pairs:
                    relay_cross(p)

    arrive(0)
    preconds = []
    weave(precondition(0, preconds))
    for p in range(max(pairs, 4)):
        relay_at(p)
        if p >= pairs:
            continue
        later = []
        streams = [solve(p, preconds)]
        if p + 1 < pairs:
            arrive(p + 1)
            streams.append(precondition(p + 1, later))
        weave(*streams)
        preconds = later

    def read_pair(p, carry):
        @pl.when(gets_side)
        def _():
            cross_across(p, cross_in).wait_recv()

        for k in range(2):
            h = 2 * p + k
            cols = pl.ds(pl.multiple_of(h * dim, dim), dim)
            own = cross_in[p] + jnp.where(lane == 1, cross_half[p], 0.0)
            prior = jnp.where(lane == k, own, cross_side[p])
            for s in range(2):
                rows = slice(s * sub, (s + 1) * sub)
                values = value_ref[rows, cols]
                final[k, s, :sub] = jnp.concatenate([values, jnp.zeros_like(values)], axis=1)
                matrix = prior if s == 0 else prior + cross_head[h]
                final[k, s, sub:] = twice(halves(matrix))
                split = solved[h, rows]
                scores = mm(split[:, :dim], turned_keys[h, :, rows])
                scores = jnp.where(causal, scores, 0.0).astype(BF16)
                total = mm(jnp.concatenate([scores, split], axis=1), final[k, s])
                out_ref[rows, cols] = fold(total).astype(BF16)
        return carry

    lax.fori_loop(0, pairs, read_pair, 0)

    for p in range(pairs):
        cross_swap(p).wait_send()

        @pl.when(has_next)
        def _():
            for q in range(2):
                gram_next(p, q).wait_send()
            cross_next(p).wait_send()

        @pl.when(jnp.logical_or(lane == 0, has_prev))
        def _():
            for q in range(2):
                gram_across(p, q, gram_out).wait_send()
            cross_across(p, cross_out).wait_send()


def solution(mesh):
    chain = mesh.shape["seq"] // LANES

    def body(query_rows, key_rows, value_rows, key_gain, regularizer):
        heads = key_gain.shape[0]
        tokens, width = query_rows.shape
        dim = width // heads
        sub, pairs = tokens // 2, heads // 2
        vmem = pl.BlockSpec(memory_space=pltpu.VMEM)
        hbm = pl.BlockSpec(memory_space=pl.ANY)
        smem = pl.BlockSpec(memory_space=pltpu.SMEM)
        rows = pltpu.VMEM((tokens, width), BF16)
        square = pltpu.VMEM((heads, dim, dim), F32)
        packed = pltpu.VMEM((pairs, dim + 8, dim), F32)
        crosses = pltpu.VMEM((pairs, dim, dim), F32)
        return pl.pallas_call(
            functools.partial(kernel, chain),
            out_shape=jax.ShapeDtypeStruct((tokens, width), BF16),
            in_specs=[smem, smem, hbm, hbm, hbm],
            out_specs=vmem,
            scratch_shapes=[
                rows, rows, rows,
                pltpu.VMEM((heads, tokens, dim), BF16),
                pltpu.VMEM((heads, dim, tokens), BF16),
                square, square, square, square,
                packed, packed, packed,
                crosses, crosses, crosses, crosses, crosses,
                pltpu.VMEM((2, 2, 2, sub + 2 * dim, 2 * dim), BF16),
                pltpu.VMEM((2, 2, tokens, dim), F32),
                pltpu.VMEM((heads, tokens, 2 * dim), BF16),
                pltpu.VMEM((2, 2, sub + 2 * dim, 2 * dim), BF16),
            ]
            + [pltpu.SemaphoreType.DMA((pairs,)) for _ in range(3)]
            + [pltpu.SemaphoreType.DMA((2 * pairs,)) for _ in range(4)]
            + [pltpu.SemaphoreType.DMA((pairs,)) for _ in range(6)],
            compiler_params=pltpu.CompilerParams(collective_id=0, has_side_effects=True),
            name="mesa_prefill",
        )(key_gain, regularizer, query_rows, key_rows, value_rows)

    placed = (P("seq", "head"), P("seq", "head"), P("seq", "head"), P("head"), P("head"))
    return jax.shard_map(
        body, mesh=mesh, in_specs=placed, out_specs=P("seq", "head"), check_vma=False
    )
```

profile of v0, /device:TPU:26, one launch (start us, length us, event | category | flops | bytes accessed | tf_op | source)
XLA Modules:
  0.0 35.1 jit_solution(699526622036219254)
XLA Ops:
  0.0 32.9 %mesa_prefill.1 = bf16[512,1024]{1,0:T(8,128)(2,1)} custom-call(f32[8]{0:T(128)} %gain_ref.1, f32[8]{0:T(128)} %ridge_ref.1, bf16[512,1024]{1,0:T(8,128)(2,1)} %query_hbm.1, bf16[512,1024]{1,0:T(8,128)(2,1)} %key_hbm.1, bf16[512,1024]{1,0:T(8,128)(2,1)} %value_hbm.1), custom_call_target="tpu_custom_call" | custom-call | tf_op jit(solution)/shard_map/mesa_prefill/pallas_call | solution.py:388
  32.9 2.3 %copy.7 = bf16[512,1024]{1,0:T(8,128)(2,1)} copy(bf16[512,1024]{1,0:T(8,128)(2,1)} %mesa_prefill.1) | data formatting | bytes 2097152
where the time goes:
time: 35.3 us; the launch traced here: 35.1 us
  Pallas kernels  32.9 us (93%)
  local copies, waits for them, and re-layouts  2.26 us (6%)
    pallas_call x1, Pallas kernels, body(): pl.pallas_call(functools.partial(kernel, chain), out_shape=jax.ShapeDtype...  32.9 us
    unnamed x1, local copies, waits for them, and re-layouts  2.26 us

commit v1 on v0

--- a/solution.py
+++ b/solution.py
@@ -387,7 +387,7 @@
         crosses = pltpu.VMEM((pairs, dim, dim), F32)
         return pl.pallas_call(
             functools.partial(kernel, chain),
-            out_shape=jax.ShapeDtypeStruct((tokens, width), BF16),
+            out_shape=pltpu.VMEM((tokens, width), BF16),
             in_specs=[smem, smem, hbm, hbm, hbm],
             out_specs=vmem,
             scratch_shapes=[

time: 35.3 us -> 33 us (0.935)
  local copies, waits for them, and re-layouts: 2.26 us -> 0.97 us
  Pallas kernels: 32.9 us -> 31.9 us
    unnamed x1, local copies, waits for them, and re-layouts: 2.26 us -> 0.97 us
    pallas_call x1, Pallas kernels: 32.9 us -> 31.9 us  [body(): pl.pallas_call(functools.partial(kernel, chain), out_shape=pltpu.VMEM((to...]
where the time goes in v1:
time: 33 us; the launch traced here: 32.9 us
  Pallas kernels  31.9 us (97%)
  local copies, waits for them, and re-layouts  0.97 us (3%)
    pallas_call x1, Pallas kernels, body(): pl.pallas_call(functools.partial(kernel, chain), out_shape=pltpu.VMEM((to...  31.9 us
    unnamed x1, local copies, waits for them, and re-layouts  0.97 us

profile of v1, /device:TPU:26, one launch (start us, length us, event | category | flops | bytes accessed | tf_op | source)
XLA Modules:
  0.0 32.9 jit_solution(17942254719719134697)
XLA Ops:
  0.0 31.9 %mesa_prefill.1 = bf16[512,1024]{1,0:T(8,128)(2,1)S(1)} custom-call(f32[8]{0:T(128)} %gain_ref.1, f32[8]{0:T(128)} %ridge_ref.1, bf16[512,1024]{1,0:T(8,128)(2,1)} %query_hbm.1, bf16[512,1024]{1,0:T(8,128)(2,1)} %key_hbm.1, bf16[512,1024]{1,0:T(8,128)(2,1)} %value_hbm.1), custom_call_target="tpu_custom_call" | custom-call | tf_op jit(solution)/shard_map/mesa_prefill/pallas_call | solution.py:388
  31.9 1.0 %copy.7 = bf16[512,1024]{1,0:T(8,128)(2,1)} copy(bf16[512,1024]{1,0:T(8,128)(2,1)S(1)} %mesa_prefill.1) | data formatting | bytes 2097152

commit v2 on v1

--- a/solution.py
+++ b/solution.py
@@ -101,20 +101,29 @@
             device_id={"seq": device}, device_id_type=MESH,
         )
 
-    pieces = [(p, q) for p in range(pairs) for q in range(2)]
-    spans = (slice(0, dim // 2), slice(dim // 2, dim + 8))
+    first_row = jnp.logical_not(has_prev)
+    last_row = jnp.logical_and(has_prev, jnp.logical_not(has_next))
+    middle = jnp.logical_and(has_prev, has_next)
+    cuts = [dim // 4, dim // 2, 3 * dim // 4, dim + 8]
+    quarters = [slice(a, b) for a, b in zip([0] + cuts[:-1], cuts)]
+    halved = [slice(0, cuts[1]), slice(cuts[1], cuts[3])]
+    spans = {(p, q): span for p in range(pairs) for q, span in enumerate(halved if p else quarters)}
+    number = {piece: n for n, piece in enumerate(spans)}
+
+    def pieces(p):
+        return [q for k, q in spans if k == p]
 
     def gram_next(p, q):
-        n = 2 * p + q
+        n = number[p, q]
         return copy(
-            gram_out.at[p, spans[q]], gram_in.at[p, spans[q]],
+            gram_out.at[p, spans[p, q]], gram_in.at[p, spans[p, q]],
             gram_send.at[n], gram_recv.at[n], place + LANES,
         )
 
     def gram_across(p, q, src):
-        n = 2 * p + q
+        n = number[p, q]
         return copy(
-            src.at[p, spans[q]], gram_side.at[p, spans[q]],
+            src.at[p, spans[p, q]], gram_side.at[p, spans[p, q]],
             side_send.at[n], side_recv.at[n], partner,
         )
 
@@ -124,14 +133,29 @@
     def cross_across(p, src):
         return copy(src.at[p], cross_side.at[p], cside_send.at[p], cside_recv.at[p], partner)
 
-    def send_gram(p, q):
-        @pl.when(has_next)
-        def _():
-            gram_next(p, q).start()
-
-        @pl.when(lane == 0)
-        def _():
-            gram_across(p, q, gram_out).start()
+    def send_side(p):
+        @pl.when(jnp.logical_and(first_row, lane == 0))
+        def _():
+            for q in pieces(p):
+                gram_across(p, q, gram_out).start()
+
+    def relay_gram(p):
+        for q in pieces(p):
+            gram_next(p, q).wait_recv()
+
+            @pl.when(lane == 1)
+            def _():
+                gram_across(p, q, gram_in).start()
+
+            gram_out[p, spans[p, q]] += gram_in[p, spans[p, q]]
+
+            @pl.when(has_next)
+            def _():
+                gram_next(p, q).start()
+
+            @pl.when(lane == 0)
+            def _():
+                gram_across(p, q, gram_out).start()
 
     def cross_swap(p):
         return copy(
@@ -180,10 +204,13 @@
         if p == 0:
             pl.semaphore_wait(barrier, 1 + has_prev.astype(jnp.int32) + has_next.astype(jnp.int32))
 
-        @pl.when(jnp.logical_not(has_prev))
-        def _():
-            for q in range(2):
-                send_gram(p, q)
+        @pl.when(jnp.logical_and(first_row, has_next))
+        def _():
+            for q in pieces(p):
+                gram_next(p, q).start()
+
+        if p == 0:
+            send_side(p)
 
     for p in range(pairs):
         fetch(p, value_hbm, value_ref, value_sem).wait()
@@ -193,14 +220,21 @@
             total = first + mm(turned_keys[h, :, sub:], values[sub:])
             cross_head[h] = first
             cross_all[h] = total
-        cross_swap(p).start()
-
-    @pl.when(jnp.logical_not(has_prev))
+        if p < 2:
+            cross_swap(p).start()
+        else:
+            @pl.when(jnp.logical_not(middle))
+            def _():
+                cross_swap(p).start()
+        if p == 1:
+            send_side(1)
+    for p in range(2, pairs):
+        send_side(p)
+
+    @pl.when(first_row)
     def _():
         gram_in[...] = jnp.zeros_like(gram_in)
         cross_in[...] = jnp.zeros_like(cross_in)
-        for p in range(pairs):
-            relay_cross(p)
 
     @pl.when(jnp.logical_not(gets_side))
     def _():
@@ -210,22 +244,22 @@
     for p in range(pairs):
         fetch(p, query_hbm, query_ref, query_sem).wait()
 
-    @pl.when(has_prev)
-    def _():
-        for p, q in pieces:
-            gram_next(p, q).wait_recv()
-
-            @pl.when(lane == 1)
-            def _():
-                gram_across(p, q, gram_in).start()
-
-            gram_out[p, spans[q]] += gram_in[p, spans[q]]
-            send_gram(p, q)
+    @pl.when(middle)
+    def _():
+        for p in range(pairs):
+            relay_gram(p)
+            if 1 <= p < pairs - 1:
+                cross_swap(p + 1).start()
+
+    @pl.when(last_row)
+    def _():
+        for p in range(min(2, pairs)):
+            relay_gram(p)
 
     def arrive(p):
         @pl.when(gets_side)
         def _():
-            for q in range(2):
+            for q in pieces(p):
                 gram_across(p, q, gram_in).wait_recv()
 
     def precondition(p, result):
@@ -297,36 +331,42 @@
         while streams:
             streams = [stream for stream in streams if next(stream, 0) is None]
 
-    def relay_at(stage):
-        early = {0: (0, 1), 1: (2,), 2: range(3, pairs)}
-        late = {1: (0,), 2: (1,), 3: range(2, pairs)}
-        mine, spare = early.get(stage, ()), late.get(stage, ())
-
-        @pl.when(jnp.logical_and(has_prev, has_next))
-        def _():
-            for p in mine:
-                if p < pairs:
-                    relay_cross(p)
-
-        @pl.when(jnp.logical_and(has_prev, jnp.logical_not(has_next)))
-        def _():
-            for p in spare:
-                if p < pairs:
-                    relay_cross(p)
+    rows = jnp.minimum(row, 2)
+    roles = (
+        (first_row, (0, 0, 0, 0)),
+        (jnp.logical_and(middle, rows == 1), (0, 0, 0, 1)),
+        (jnp.logical_and(middle, rows == 2), (0, 1, 1, 2)),
+        (last_row, (1, 2, 2, 3)),
+    )
+    end = pairs
+
+    def relay_at(slot):
+        for role, slots in roles:
+            units = [p for p in range(pairs) if min(slots[min(p, 3)], end) == slot]
+            if units:
+                @pl.when(role)
+                def _():
+                    for p in units:
+                        relay_cross(p)
 
     arrive(0)
     preconds = []
     weave(precondition(0, preconds))
-    for p in range(max(pairs, 4)):
-        relay_at(p)
-        if p >= pairs:
-            continue
+
+    @pl.when(last_row)
+    def _():
+        for p in range(2, pairs):
+            relay_gram(p)
+
+    relay_at(0)
+    for p in range(pairs):
         later = []
         streams = [solve(p, preconds)]
         if p + 1 < pairs:
             arrive(p + 1)
             streams.append(precondition(p + 1, later))
         weave(*streams)
+        relay_at(p + 1)
         preconds = later
 
     def read_pair(p, carry):
@@ -359,13 +399,13 @@
 
         @pl.when(has_next)
         def _():
-            for q in range(2):
+            for q in pieces(p):
                 gram_next(p, q).wait_send()
             cross_next(p).wait_send()
 
         @pl.when(jnp.logical_or(lane == 0, has_prev))
         def _():
-            for q in range(2):
+            for q in pieces(p):
                 gram_across(p, q, gram_out).wait_send()
             cross_across(p, cross_out).wait_send()
 
@@ -403,7 +443,7 @@
                 pltpu.VMEM((2, 2, sub + 2 * dim, 2 * dim), BF16),
             ]
             + [pltpu.SemaphoreType.DMA((pairs,)) for _ in range(3)]
-            + [pltpu.SemaphoreType.DMA((2 * pairs,)) for _ in range(4)]
+            + [pltpu.SemaphoreType.DMA((2 * pairs + 2,)) for _ in range(4)]
             + [pltpu.SemaphoreType.DMA((pairs,)) for _ in range(6)],
             compiler_params=pltpu.CompilerParams(collective_id=0, has_side_effects=True),
             name="mesa_prefill",

time: 33 us -> 30.1 us (0.912)
  Pallas kernels: 31.9 us -> 28.9 us
    pallas_call x1, Pallas kernels: 31.9 us -> 28.9 us  [body(): pl.pallas_call(functools.partial(kernel, chain), out_shape=pltpu.VMEM((to...]
where the time goes in v2:
time: 30.1 us; the launch traced here: 29.9 us
  Pallas kernels  28.9 us (96%)
  local copies, waits for them, and re-layouts  0.97 us (3%)
    pallas_call x1, Pallas kernels, body(): pl.pallas_call(functools.partial(kernel, chain), out_shape=pltpu.VMEM((to...  28.9 us
    unnamed x1, local copies, waits for them, and re-layouts  0.97 us

profile of v2, /device:TPU:26, one launch (start us, length us, event | category | flops | bytes accessed | tf_op | source)
XLA Modules:
  0.0 29.9 jit_solution(5064101748482526375)
XLA Ops:
  0.0 28.9 %mesa_prefill.1 = bf16[512,1024]{1,0:T(8,128)(2,1)S(1)} custom-call(f32[8]{0:T(128)} %gain_ref.1, f32[8]{0:T(128)} %ridge_ref.1, bf16[512,1024]{1,0:T(8,128)(2,1)} %query_hbm.1, bf16[512,1024]{1,0:T(8,128)(2,1)} %key_hbm.1, bf16[512,1024]{1,0:T(8,128)(2,1)} %value_hbm.1), custom_call_target="tpu_custom_call" | custom-call | tf_op jit(solution)/shard_map/mesa_prefill/pallas_call | solution.py:428
  28.9 1.0 %copy.7 = bf16[512,1024]{1,0:T(8,128)(2,1)} copy(bf16[512,1024]{1,0:T(8,128)(2,1)S(1)} %mesa_prefill.1) | data formatting | bytes 2097152

commit v3 on v2

--- a/solution.py
+++ b/solution.py
@@ -10,6 +10,8 @@
 NS_STEPS = 8
 REFINE = 2
 LANES = 2
+PARTS = 4
+GROUP = 1
 F32 = jnp.float32
 BF16 = jnp.bfloat16
 MESH = pl.DeviceIdType.MESH
@@ -44,18 +46,18 @@
 
 def kernel(
     chain,
-    gain_ref, ridge_ref, query_hbm, key_hbm, value_hbm, out_ref,
+    gain_hbm, ridge_hbm, query_hbm, key_hbm, value_hbm, out_ref,
+    gain_ref, ridge_ref,
     query_ref, key_ref, value_ref,
-    keys, turned_keys, gram_head, gram_all, cross_head, cross_all,
+    keys, turned_keys, gram_parts, gram_all, cross_head, cross_all,
     gram_in, gram_out, gram_side, cross_in, cross_out, cross_mix, cross_half, cross_side,
     weights, start, solved, final,
-    query_sem, key_sem, value_sem,
+    query_sem, key_sem, value_sem, gain_sem, ridge_sem,
     gram_send, gram_recv, side_send, side_recv,
     cross_send, cross_recv, half_send, half_recv, cside_send, cside_recv,
 ):
-    heads = keys.shape[0]
-    tokens, dim = keys.shape[1:]
-    sub = tokens // 2
+    heads, dim, tokens = turned_keys.shape
+    sub, part = tokens // 2, tokens // PARTS
     pairs = heads // 2
     place = lax.axis_index("seq")
     row, lane = place // LANES, place % LANES
@@ -84,8 +86,13 @@
     def fetch(p, src, dst, sem):
         return pltpu.make_async_copy(src.at[:, pair_cols(p)], dst.at[:, pair_cols(p)], sem.at[p])
 
-    for p in range(pairs):
+    gains = pltpu.make_async_copy(gain_hbm, gain_ref, gain_sem)
+    ridges = pltpu.make_async_copy(ridge_hbm, ridge_ref, ridge_sem)
+    fetch(0, key_hbm, key_ref, key_sem).start()
+    gains.start()
+    for p in range(1, pairs):
         fetch(p, key_hbm, key_ref, key_sem).start()
+    ridges.start()
     for p in range(pairs):
         fetch(p, value_hbm, value_ref, value_sem).start()
     for p in range(pairs):
@@ -163,8 +170,15 @@
             half_send.at[p], half_recv.at[p], partner,
         )
 
+    def swap_cross(p):
+        @pl.when(jnp.logical_not(jnp.logical_and(last_row, lane == 1)))
+        def _():
+            cross_swap(p).start()
+
     def relay_cross(p):
-        cross_swap(p).wait_recv()
+        @pl.when(jnp.logical_not(jnp.logical_and(last_row, lane == 0)))
+        def _():
+            cross_swap(p).wait_recv()
 
         @pl.when(has_prev)
         def _():
@@ -186,17 +200,16 @@
             cross_out[p] = mixed + cross_half[p]
             cross_next(p).start()
 
+    gains.wait()
     for p in range(pairs):
         fetch(p, key_hbm, key_ref, key_sem).wait()
         for h in (2 * p, 2 * p + 1):
             raw = key_ref[:, h * dim : (h + 1) * dim].astype(F32)
             scaled = (raw * gain_ref[h]).astype(BF16)
             turned = scaled.T
-            keys[h] = scaled
+            keys[p, :, (h - 2 * p) * dim : (h - 2 * p + 1) * dim] = scaled
             turned_keys[h] = turned
-            first = mm(turned[:, :sub], scaled[:sub])
-            gram_head[h] = first
-            gram_all[h] = first + mm(turned[:, sub:], scaled[sub:])
+            gram_all[h] = mm(turned, scaled)
         upper, lower = gram_all[2 * p], gram_all[2 * p + 1]
         gram_out[p, :dim] = jnp.where(i <= j, upper, lower)
         diagonal = jnp.sum(jnp.where(i == j, lower, 0.0), axis=0, keepdims=True)
@@ -221,11 +234,11 @@
             cross_head[h] = first
             cross_all[h] = total
         if p < 2:
-            cross_swap(p).start()
+            swap_cross(p)
         else:
             @pl.when(jnp.logical_not(middle))
             def _():
-                cross_swap(p).start()
+                swap_cross(p)
         if p == 1:
             send_side(1)
     for p in range(2, pairs):
@@ -236,19 +249,44 @@
         gram_in[...] = jnp.zeros_like(gram_in)
         cross_in[...] = jnp.zeros_like(cross_in)
 
+    @pl.when(jnp.logical_and(last_row, lane == 0))
+    def _():
+        cross_half[...] = jnp.zeros_like(cross_half)
+
     @pl.when(jnp.logical_not(gets_side))
     def _():
         gram_side[...] = jnp.zeros_like(gram_side)
         cross_side[...] = jnp.zeros_like(cross_side)
 
+    ridges.wait()
     for p in range(pairs):
         fetch(p, query_hbm, query_ref, query_sem).wait()
 
+    second_row = jnp.logical_and(middle, row == 1)
+
+    @pl.when(second_row)
+    def _():
+        relay_gram(0)
+
+    weights[:, :, :, :part, dim:] = jnp.zeros((2, 2, PARTS, part, dim), BF16)
+    for h in range(heads):
+        total = None
+        for s in range(PARTS - 1):
+            rows = slice(s * part, (s + 1) * part)
+            cols = slice(h % 2 * dim, (h % 2 + 1) * dim)
+            gram = mm(turned_keys[h, :, rows], keys[h // 2, rows, cols])
+            total = gram if total is None else total + gram
+            gram_parts[h, s * dim : (s + 1) * dim] = halves(total)
+
+    @pl.when(jnp.logical_and(middle, row > 1))
+    def _():
+        relay_gram(0)
+
     @pl.when(middle)
     def _():
-        for p in range(pairs):
+        for p in range(1, pairs):
             relay_gram(p)
-            if 1 <= p < pairs - 1:
+            if p < pairs - 1:
                 cross_swap(p + 1).start()
 
     @pl.when(last_row)
@@ -271,60 +309,86 @@
         state = []
         for h, prior in ((2 * p, upper), (2 * p + 1, lower)):
             plain = ridge_ref[h] * eye + prior
-            gram_head[h] = plain + gram_head[h]
             end = plain + gram_all[h]
             gram_all[h] = plain
             total = jnp.sum(jnp.sum(end * end, axis=1, keepdims=True), axis=0, keepdims=True)
             inverse = 1.0 / jnp.sqrt(total)
             rest = eye - end * inverse
             split = halves(rest)
-            both = jnp.concatenate([eye + rest, fold(mm(split, twice(split)))], axis=0)
+            both = jnp.concatenate([fold(mm(split, twice(split))), eye + rest], axis=0)
             state.append((both, inverse))
         yield
         for step in range(NS_STEPS - 2):
             for k in range(2):
                 both, inverse = state[k]
                 split = halves(both)
-                product = fold(mm(split, twice(split[dim:])))
-                both = jnp.concatenate([both[:dim] + product[:dim], product[dim:]], axis=0)
+                product = fold(mm(split, twice(split[:dim])))
+                both = jnp.concatenate([product[:dim], both[dim:] + product[dim:]], axis=0)
                 state[k] = (both, inverse)
             yield
         for both, inverse in state:
             split = halves(both)
-            approx = both[:dim] + fold(mm(split[:dim], twice(split[dim:])))
+            approx = both[dim:] + fold(mm(split[dim:], twice(split[:dim])))
             result.append(halves(approx * inverse))
         yield
 
-    t = lax.broadcasted_iota(jnp.int32, (sub, sub), 0)
-    u = lax.broadcasted_iota(jnp.int32, (sub, sub), 1)
-    causal = t >= u
+    def causal(size):
+        t = lax.broadcasted_iota(jnp.int32, (size, size), 0)
+        u = lax.broadcasted_iota(jnp.int32, (size, size), 1)
+        return t >= u
 
     def solve(p, preconds):
         slot = p % 2
-        for k in range(2):
+        blank = jnp.zeros((dim, dim), BF16)
+        both = jnp.concatenate([
+            jnp.concatenate([preconds[0][:, :dim], blank], axis=1),
+            jnp.concatenate([blank, preconds[1][:, :dim]], axis=1),
+        ], axis=0)
+        shifted = (-mm(keys[p], both)).astype(BF16)
+        scores, current = {}, {}
+
+        def prepare(k):
             h = 2 * p + k
             precond = preconds[k]
             start[slot, k] = fold(mm(query_ref[:, h * dim : (h + 1) * dim], precond))
-            shifted = halves(-fold(mm(keys[h], precond)))
-            for s, matrix in ((0, gram_all), (1, gram_head)):
-                rest = halves(eye - fold(mm(halves(matrix[h]), twice(precond))))
-                weights[slot, k, s, :sub] = shifted[s * sub : (s + 1) * sub]
-                weights[slot, k, s, sub:] = twice(rest)
+            stack = jnp.concatenate([halves(gram_all[h]), gram_parts[h]], axis=0)
+            product = fold(mm(stack, twice(precond)))
+            rest = eye - product[:dim]
+            for s in range(PARTS):
+                left = rest - product[s * dim : (s + 1) * dim] if s else rest
+                weights[slot, k, s, :part, :dim] = shifted[s * part : (s + 1) * part, k * dim : (k + 1) * dim]
+                weights[slot, k, s, part:] = halves(left)
+                current[k, s] = start[slot, k, s * part : (s + 1) * part].astype(BF16)
+
+        def score(k):
+            for s in range(PARTS):
+                product = mm(current[k, s], turned_keys[2 * p + k, :, s * part : (s + 1) * part])
+                scores[k, s] = jnp.where(causal(part), product, 0.0).astype(BF16)
+
+        def update(k, last):
+            for s in range(PARTS):
+                rows = slice(s * part, (s + 1) * part)
+                both = jnp.concatenate([scores[k, s], current[k, s]], axis=1)
+                value = start[slot, k, rows] + fold(mm(both, weights[slot, k, s]))
+                if last:
+                    solved[2 * p + k, rows] = halves(value)
+                else:
+                    current[k, s] = value.astype(BF16)
+
+        prepare(0)
+        yield
+        prepare(1)
+        score(0)
+        yield
+        for repeat in range(REFINE):
+            last = repeat == REFINE - 1
+            update(0, last)
+            score(1)
             yield
-        chains = [(k, s) for k in range(2) for s in range(2)]
-        current = {(k, s): start[slot, k, s * sub : (s + 1) * sub] for k, s in chains}
-        for repeat in range(REFINE):
-            for k, s in chains:
-                rows = slice(s * sub, (s + 1) * sub)
-                split = halves(current[k, s])
-                scores = mm(split[:, :dim], turned_keys[2 * p + k, :, rows])
-                scores = jnp.where(causal, scores, 0.0).astype(BF16)
-                update = mm(jnp.concatenate([scores, split], axis=1), weights[slot, k, s])
-                current[k, s] = start[slot, k, rows] + fold(update)
-                if s == 1:
-                    yield
-        for k, s in chains:
-            solved[2 * p + k, s * sub : (s + 1) * sub] = halves(current[k, s])
+            update(1, last)
+            if not last:
+                score(0)
+            yield
 
     def weave(*streams):
         streams = list(streams)
@@ -350,12 +414,18 @@
                         relay_cross(p)
 
     arrive(0)
+
+    @pl.when(last_row)
+    def _():
+        for p in range(2, min(3, pairs)):
+            relay_gram(p)
+
     preconds = []
     weave(precondition(0, preconds))
 
     @pl.when(last_row)
     def _():
-        for p in range(2, pairs):
+        for p in range(3, pairs):
             relay_gram(p)
 
     relay_at(0)
@@ -369,12 +439,14 @@
         relay_at(p + 1)
         preconds = later
 
-    def read_pair(p, carry):
-        @pl.when(gets_side)
-        def _():
-            cross_across(p, cross_in).wait_recv()
-
-        for k in range(2):
+    def read(turn, carry):
+        for n in range(GROUP):
+            @pl.when(gets_side)
+            def _():
+                cross_across(turn * GROUP + n, cross_in).wait_recv()
+
+        for n, k in [(n, k) for n in range(GROUP) for k in range(2)]:
+            p = turn * GROUP + n
             h = 2 * p + k
             cols = pl.ds(pl.multiple_of(h * dim, dim), dim)
             own = cross_in[p] + jnp.where(lane == 1, cross_half[p], 0.0)
@@ -382,20 +454,22 @@
             for s in range(2):
                 rows = slice(s * sub, (s + 1) * sub)
                 values = value_ref[rows, cols]
-                final[k, s, :sub] = jnp.concatenate([values, jnp.zeros_like(values)], axis=1)
+                final[n, k, s, :sub] = jnp.concatenate([values, jnp.zeros_like(values)], axis=1)
                 matrix = prior if s == 0 else prior + cross_head[h]
-                final[k, s, sub:] = twice(halves(matrix))
+                final[n, k, s, sub:] = twice(halves(matrix))
                 split = solved[h, rows]
                 scores = mm(split[:, :dim], turned_keys[h, :, rows])
-                scores = jnp.where(causal, scores, 0.0).astype(BF16)
-                total = mm(jnp.concatenate([scores, split], axis=1), final[k, s])
+                scores = jnp.where(causal(sub), scores, 0.0).astype(BF16)
+                total = mm(jnp.concatenate([scores, split], axis=1), final[n, k, s])
                 out_ref[rows, cols] = fold(total).astype(BF16)
         return carry
 
-    lax.fori_loop(0, pairs, read_pair, 0)
-
-    for p in range(pairs):
-        cross_swap(p).wait_send()
+    lax.fori_loop(0, pairs // GROUP, read, 0)
+
+    for p in range(pairs):
+        @pl.when(jnp.logical_not(jnp.logical_and(last_row, lane == 1)))
+        def _():
+            cross_swap(p).wait_send()
 
         @pl.when(has_next)
         def _():
@@ -420,7 +494,6 @@
         sub, pairs = tokens // 2, heads // 2
         vmem = pl.BlockSpec(memory_space=pltpu.VMEM)
         hbm = pl.BlockSpec(memory_space=pl.ANY)
-        smem = pl.BlockSpec(memory_space=pltpu.SMEM)
         rows = pltpu.VMEM((tokens, width), BF16)
         square = pltpu.VMEM((heads, dim, dim), F32)
         packed = pltpu.VMEM((pairs, dim + 8, dim), F32)
@@ -428,21 +501,24 @@
         return pl.pallas_call(
             functools.partial(kernel, chain),
             out_shape=pltpu.VMEM((tokens, width), BF16),
-            in_specs=[smem, smem, hbm, hbm, hbm],
+            in_specs=[hbm] * 5,
             out_specs=vmem,
             scratch_shapes=[
+                pltpu.SMEM((heads,), F32), pltpu.SMEM((heads,), F32),
                 rows, rows, rows,
-                pltpu.VMEM((heads, tokens, dim), BF16),
+                pltpu.VMEM((pairs, tokens, 2 * dim), BF16),
                 pltpu.VMEM((heads, dim, tokens), BF16),
-                square, square, square, square,
+                pltpu.VMEM((heads, (PARTS - 1) * dim, 2 * dim), BF16),
+                square, square, square,
                 packed, packed, packed,
                 crosses, crosses, crosses, crosses, crosses,
-                pltpu.VMEM((2, 2, 2, sub + 2 * dim, 2 * dim), BF16),
+                pltpu.VMEM((2, 2, PARTS, tokens // PARTS + dim, 2 * dim), BF16),
                 pltpu.VMEM((2, 2, tokens, dim), F32),
                 pltpu.VMEM((heads, tokens, 2 * dim), BF16),
-                pltpu.VMEM((2, 2, sub + 2 * dim, 2 * dim), BF16),
+                pltpu.VMEM((GROUP, 2, 2, sub + 2 * dim, 2 * dim), BF16),
             ]
             + [pltpu.SemaphoreType.DMA((pairs,)) for _ in range(3)]
+            + [pltpu.SemaphoreType.DMA] * 2
             + [pltpu.SemaphoreType.DMA((2 * pairs + 2,)) for _ in range(4)]
             + [pltpu.SemaphoreType.DMA((pairs,)) for _ in range(6)],
             compiler_params=pltpu.CompilerParams(collective_id=0, has_side_effects=True),

time: 30.1 us -> 28.4 us (0.944)
  Pallas kernels: 28.9 us -> 27.3 us
    pallas_call x1, Pallas kernels: 28.9 us -> 27.3 us  [body(): pl.pallas_call(functools.partial(kernel, chain), out_shape=pltpu.VMEM((to...]
where the time goes in v3:
time: 28.4 us; the launch traced here: 28.3 us
  Pallas kernels  27.3 us (96%)
  local copies, waits for them, and re-layouts  0.97 us (3%)
    pallas_call x1, Pallas kernels, body(): pl.pallas_call(functools.partial(kernel, chain), out_shape=pltpu.VMEM((to...  27.3 us
    unnamed x1, local copies, waits for them, and re-layouts  0.97 us

profile of v3, /device:TPU:26, one launch (start us, length us, event | category | flops | bytes accessed | tf_op | source)
XLA Modules:
  0.0 28.3 jit_solution(8127289322826019479)
XLA Ops:
  0.0 27.3 %mesa_prefill.1 = bf16[512,1024]{1,0:T(8,128)(2,1)S(1)} custom-call(f32[8]{0:T(128)} %gain_hbm.1, f32[8]{0:T(128)} %ridge_hbm.1, bf16[512,1024]{1,0:T(8,128)(2,1)} %query_hbm.1, bf16[512,1024]{1,0:T(8,128)(2,1)} %key_hbm.1, bf16[512,1024]{1,0:T(8,128)(2,1)} %value_hbm.1), custom_call_target="tpu_custom_call" | custom-call | tf_op jit(solution)/shard_map/mesa_prefill/pallas_call | solution.py:501
  27.3 1.0 %copy.7 = bf16[512,1024]{1,0:T(8,128)(2,1)} copy(bf16[512,1024]{1,0:T(8,128)(2,1)S(1)} %mesa_prefill.1) | data formatting | bytes 2097152

commit v4 on v3

--- a/solution.py
+++ b/solution.py
@@ -93,10 +93,10 @@
     for p in range(1, pairs):
         fetch(p, key_hbm, key_ref, key_sem).start()
     ridges.start()
-    for p in range(pairs):
-        fetch(p, value_hbm, value_ref, value_sem).start()
-    for p in range(pairs):
-        fetch(p, query_hbm, query_ref, query_sem).start()
+    values_in = pltpu.make_async_copy(value_hbm, value_ref, value_sem)
+    queries_in = pltpu.make_async_copy(query_hbm, query_ref, query_sem)
+    values_in.start()
+    queries_in.start()
 
     i = lax.broadcasted_iota(jnp.int32, (dim, dim), 0)
     j = lax.broadcasted_iota(jnp.int32, (dim, dim), 1)
@@ -124,21 +124,23 @@
         n = number[p, q]
         return copy(
             gram_out.at[p, spans[p, q]], gram_in.at[p, spans[p, q]],
-            gram_send.at[n], gram_recv.at[n], place + LANES,
+            gram_send, gram_recv.at[n], place + LANES,
         )
 
     def gram_across(p, q, src):
-        n = number[p, q]
         return copy(
             src.at[p, spans[p, q]], gram_side.at[p, spans[p, q]],
-            side_send.at[n], side_recv.at[n], partner,
+            side_send, side_recv.at[p], partner,
         )
 
+    def side_of(p):
+        return copy(gram_out.at[p], gram_side.at[p], side_send, side_recv.at[p], partner)
+
     def cross_next(p):
-        return copy(cross_out.at[p], cross_in.at[p], cross_send.at[p], cross_recv.at[p], place + LANES)
+        return copy(cross_out.at[p], cross_in.at[p], cross_send, cross_recv.at[p], place + LANES)
 
     def cross_across(p, src):
-        return copy(src.at[p], cross_side.at[p], cside_send.at[p], cside_recv.at[p], partner)
+        return copy(src.at[p], cross_side.at[p], cside_send, cside_recv.at[p], partner)
 
     def send_side(p):
         @pl.when(jnp.logical_and(first_row, lane == 0))
@@ -167,7 +169,7 @@
     def cross_swap(p):
         return copy(
             cross_all.at[2 * p + 1 - lane], cross_half.at[p],
-            half_send.at[p], half_recv.at[p], partner,
+            half_send, half_recv.at[p], partner,
         )
 
     def swap_cross(p):
@@ -225,8 +227,8 @@
         if p == 0:
             send_side(p)
 
+    values_in.wait()
     for p in range(pairs):
-        fetch(p, value_hbm, value_ref, value_sem).wait()
         for h in (2 * p, 2 * p + 1):
             values = value_ref[:, h * dim : (h + 1) * dim]
             first = mm(turned_keys[h, :, :sub], values[:sub])
@@ -239,9 +241,7 @@
             @pl.when(jnp.logical_not(middle))
             def _():
                 swap_cross(p)
-        if p == 1:
-            send_side(1)
-    for p in range(2, pairs):
+    for p in range(1, pairs):
         send_side(p)
 
     @pl.when(first_row)
@@ -259,8 +259,7 @@
         cross_side[...] = jnp.zeros_like(cross_side)
 
     ridges.wait()
-    for p in range(pairs):
-        fetch(p, query_hbm, query_ref, query_sem).wait()
+    queries_in.wait()
 
     second_row = jnp.logical_and(middle, row == 1)
 
@@ -297,8 +296,7 @@
     def arrive(p):
         @pl.when(gets_side)
         def _():
-            for q in pieces(p):
-                gram_across(p, q, gram_in).wait_recv()
+            side_of(p).wait_recv()
 
     def precondition(p, result):
         packed = gram_in[p] + gram_side[p]
@@ -466,22 +464,19 @@
 
     lax.fori_loop(0, pairs // GROUP, read, 0)
 
-    for p in range(pairs):
-        @pl.when(jnp.logical_not(jnp.logical_and(last_row, lane == 1)))
-        def _():
-            cross_swap(p).wait_send()
-
-        @pl.when(has_next)
-        def _():
-            for q in pieces(p):
-                gram_next(p, q).wait_send()
-            cross_next(p).wait_send()
-
-        @pl.when(jnp.logical_or(lane == 0, has_prev))
-        def _():
-            for q in pieces(p):
-                gram_across(p, q, gram_out).wait_send()
-            cross_across(p, cross_out).wait_send()
+    @pl.when(jnp.logical_not(jnp.logical_and(last_row, lane == 1)))
+    def _():
+        copy(cross_out, cross_half, half_send, half_recv.at[0], partner).wait_send()
+
+    @pl.when(has_next)
+    def _():
+        copy(gram_out, gram_in, gram_send, gram_recv.at[0], place + LANES).wait_send()
+        copy(cross_out, cross_in, cross_send, cross_recv.at[0], place + LANES).wait_send()
+
+    @pl.when(jnp.logical_or(lane == 0, has_prev))
+    def _():
+        copy(gram_out, gram_side, side_send, side_recv.at[0], partner).wait_send()
+        copy(cross_out, cross_side, cside_send, cside_recv.at[0], partner).wait_send()
 
 
 def solution(mesh):
@@ -498,6 +493,7 @@
         square = pltpu.VMEM((heads, dim, dim), F32)
         packed = pltpu.VMEM((pairs, dim + 8, dim), F32)
         crosses = pltpu.VMEM((pairs, dim, dim), F32)
+        single = pltpu.SemaphoreType.DMA
         return pl.pallas_call(
             functools.partial(kernel, chain),
             out_shape=pltpu.VMEM((tokens, width), BF16),
@@ -517,10 +513,9 @@
                 pltpu.VMEM((heads, tokens, 2 * dim), BF16),
                 pltpu.VMEM((GROUP, 2, 2, sub + 2 * dim, 2 * dim), BF16),
             ]
-            + [pltpu.SemaphoreType.DMA((pairs,)) for _ in range(3)]
-            + [pltpu.SemaphoreType.DMA] * 2
-            + [pltpu.SemaphoreType.DMA((2 * pairs + 2,)) for _ in range(4)]
-            + [pltpu.SemaphoreType.DMA((pairs,)) for _ in range(6)],
+            + [single, pltpu.SemaphoreType.DMA((pairs,))] + [single] * 3
+            + [single, pltpu.SemaphoreType.DMA((2 * pairs + 2,))]
+            + [single, pltpu.SemaphoreType.DMA((pairs,))] * 4,
             compiler_params=pltpu.CompilerParams(collective_id=0, has_side_effects=True),
             name="mesa_prefill",
         )(key_gain, regularizer, query_rows, key_rows, value_rows)

time: 28.4 us -> 27.6 us (0.972)
  Pallas kernels: 27.3 us -> 26.4 us
    pallas_call x1, Pallas kernels: 27.3 us -> 26.4 us  [body(): pl.pallas_call(functools.partial(kernel, chain), out_shape=pltpu.VMEM((to...]
where the time goes in v4:
time: 27.6 us; the launch traced here: 27.4 us
  Pallas kernels  26.4 us (96%)
  local copies, waits for them, and re-layouts  0.97 us (4%)
    pallas_call x1, Pallas kernels, body(): pl.pallas_call(functools.partial(kernel, chain), out_shape=pltpu.VMEM((to...  26.4 us
    unnamed x1, local copies, waits for them, and re-layouts  0.97 us

profile of v4, /device:TPU:26, one launch (start us, length us, event | category | flops | bytes accessed | tf_op | source)
XLA Modules:
  0.0 27.4 jit_solution(3973635785152853033)
XLA Ops:
  0.0 26.4 %mesa_prefill.1 = bf16[512,1024]{1,0:T(8,128)(2,1)S(1)} custom-call(f32[8]{0:T(128)} %gain_hbm.1, f32[8]{0:T(128)} %ridge_hbm.1, bf16[512,1024]{1,0:T(8,128)(2,1)} %query_hbm.1, bf16[512,1024]{1,0:T(8,128)(2,1)} %key_hbm.1, bf16[512,1024]{1,0:T(8,128)(2,1)} %value_hbm.1), custom_call_target="tpu_custom_call" | custom-call | tf_op jit(solution)/shard_map/mesa_prefill/pallas_call | solution.py:497
  26.4 1.0 %copy.7 = bf16[512,1024]{1,0:T(8,128)(2,1)} copy(bf16[512,1024]{1,0:T(8,128)(2,1)S(1)} %mesa_prefill.1) | data formatting | bytes 2097152

commit v5 on v4

--- a/solution.py
+++ b/solution.py
@@ -11,7 +11,6 @@
 REFINE = 2
 LANES = 2
 PARTS = 4
-GROUP = 1
 F32 = jnp.float32
 BF16 = jnp.bfloat16
 MESH = pl.DeviceIdType.MESH
@@ -411,6 +410,32 @@
                     for p in units:
                         relay_cross(p)
 
+    def cross_arrive(p):
+        @pl.when(gets_side)
+        def _():
+            cross_across(p, cross_in).wait_recv()
+
+    def read(p):
+        for k in range(2):
+            h = 2 * p + k
+            cols = pl.ds(pl.multiple_of(h * dim, dim), dim)
+            own = cross_in[p] + jnp.where(lane == 1, cross_half[p], 0.0)
+            prior = jnp.where(lane == k, own, cross_side[p])
+            for s in range(2):
+                rows = slice(s * sub, (s + 1) * sub)
+                values = value_ref[rows, cols]
+                final[k, s, :sub] = jnp.concatenate([values, jnp.zeros_like(values)], axis=1)
+                matrix = prior if s == 0 else prior + cross_head[h]
+                final[k, s, sub:] = twice(halves(matrix))
+                split = solved[h, rows]
+                scores = mm(split[:, :dim], turned_keys[h, :, rows])
+                scores = jnp.where(causal(sub), scores, 0.0).astype(BF16)
+                total = mm(jnp.concatenate([scores, split], axis=1), final[k, s])
+                out_ref[rows, cols] = fold(total).astype(BF16)
+                yield
+
+    early = min(1, pairs - 1)
+
     arrive(0)
 
     @pl.when(last_row)
@@ -433,36 +458,20 @@
         if p + 1 < pairs:
             arrive(p + 1)
             streams.append(precondition(p + 1, later))
+        elif early:
+            cross_arrive(0)
+            streams.append(read(0))
         weave(*streams)
         relay_at(p + 1)
         preconds = later
 
-    def read(turn, carry):
-        for n in range(GROUP):
-            @pl.when(gets_side)
-            def _():
-                cross_across(turn * GROUP + n, cross_in).wait_recv()
-
-        for n, k in [(n, k) for n in range(GROUP) for k in range(2)]:
-            p = turn * GROUP + n
-            h = 2 * p + k
-            cols = pl.ds(pl.multiple_of(h * dim, dim), dim)
-            own = cross_in[p] + jnp.where(lane == 1, cross_half[p], 0.0)
-            prior = jnp.where(lane == k, own, cross_side[p])
-            for s in range(2):
-                rows = slice(s * sub, (s + 1) * sub)
-                values = value_ref[rows, cols]
-                final[n, k, s, :sub] = jnp.concatenate([values, jnp.zeros_like(values)], axis=1)
-                matrix = prior if s == 0 else prior + cross_head[h]
-                final[n, k, s, sub:] = twice(halves(matrix))
-                split = solved[h, rows]
-                scores = mm(split[:, :dim], turned_keys[h, :, rows])
-                scores = jnp.where(causal(sub), scores, 0.0).astype(BF16)
-                total = mm(jnp.concatenate([scores, split], axis=1), final[n, k, s])
-                out_ref[rows, cols] = fold(total).astype(BF16)
+    def read_pair(p, carry):
+        cross_arrive(p)
+        for _ in read(p):
+            pass
         return carry
 
-    lax.fori_loop(0, pairs // GROUP, read, 0)
+    lax.fori_loop(early, pairs, read_pair, 0)
 
     @pl.when(jnp.logical_not(jnp.logical_and(last_row, lane == 1)))
     def _():
@@ -511,7 +520,7 @@
                 pltpu.VMEM((2, 2, PARTS, tokens // PARTS + dim, 2 * dim), BF16),
                 pltpu.VMEM((2, 2, tokens, dim), F32),
                 pltpu.VMEM((heads, tokens, 2 * dim), BF16),
-                pltpu.VMEM((GROUP, 2, 2, sub + 2 * dim, 2 * dim), BF16),
+                pltpu.VMEM((2, 2, sub + 2 * dim, 2 * dim), BF16),
             ]
             + [single, pltpu.SemaphoreType.DMA((pairs,))] + [single] * 3
             + [single, pltpu.SemaphoreType.DMA((2 * pairs + 2,))]

time: 27.6 us -> 27.6 us (level)
  no operation moved by 1% of the time
where the time goes in v5:
time: 27.6 us; the launch traced here: 27.4 us
  Pallas kernels  26.4 us (96%)
  local copies, waits for them, and re-layouts  0.97 us (4%)
    pallas_call x1, Pallas kernels, body(): pl.pallas_call(functools.partial(kernel, chain), out_shape=pltpu.VMEM((to...  26.4 us
    unnamed x1, local copies, waits for them, and re-layouts  0.97 us

profile of v5, /device:TPU:26, one launch (start us, length us, event | category | flops | bytes accessed | tf_op | source)
XLA Modules:
  0.0 27.4 jit_solution(946887969951025748)
XLA Ops:
  0.0 26.4 %mesa_prefill.1 = bf16[512,1024]{1,0:T(8,128)(2,1)S(1)} custom-call(f32[8]{0:T(128)} %gain_hbm.1, f32[8]{0:T(128)} %ridge_hbm.1, bf16[512,1024]{1,0:T(8,128)(2,1)} %query_hbm.1, bf16[512,1024]{1,0:T(8,128)(2,1)} %key_hbm.1, bf16[512,1024]{1,0:T(8,128)(2,1)} %value_hbm.1), custom_call_target="tpu_custom_call" | custom-call | tf_op jit(solution)/shard_map/mesa_prefill/pallas_call | solution.py:506
  26.4 1.0 %copy.7 = bf16[512,1024]{1,0:T(8,128)(2,1)} copy(bf16[512,1024]{1,0:T(8,128)(2,1)S(1)} %mesa_prefill.1) | data formatting | bytes 2097152
